TPU v7x, 128 devices: a whole 4x4x4 slice. The times are simulated.
128 devices in a mesh: py: 8 (over y, core), px: 4 (over x), pz: 4 (over z).
Axes of the slice: x: 4, y: 4, z: 4, core: 2. Of those that a mesh axis runs over, the one named last changes fastest.
Arguments:
- tracer: float32 [128, 512, 32, 128], P('py', 'px', 'pz'), may hold values from 0.2 to 1.8
- conductance: float32 [128, 512, 32, 128], P('py', 'px', 'pz'), may hold values from 0.03 to 0.15
- source: float32 [128, 512, 32, 128], P('py', 'px', 'pz'), may hold values from -0.2 to 0.2
Outputs:
- potential: float32 [128, 512, 32, 128], P('py', 'px', 'pz')
- tracer_end: float32 [128, 512, 32, 128], P('py', 'px', 'pz')
All inputs are finite; a program needn't handle non-finite values.
Results may differ from a plain program's by a relative error of at most 0.00002.
Values sent between devices are 32-bit elements; how exact they have to be, the bound alone decides.
A program may use at most 320 MiB of HBM per device.

v0:
```python
import functools

import jax
import jax.numpy as jnp
from jax import lax
from jax.experimental import pallas as pl
from jax.experimental.pallas import tpu as pltpu
from jax.sharding import PartitionSpec as P

MESH = pl.DeviceIdType.MESH
STEPS = 4
SLAB = 8
DOWN, UP = 0, 1


def kernel(
    rows, width, zsize, total_z,
    tracer, conductance, source,
    potential, end,
    even, odd, cond, src, z_out, z_in, p_out, p_in,
    load_sem, zs, zr, xs, xr, ys, yr, ps, pr,
):
    fields = (even, odd)
    axes = ("py", "px", "pz")
    me = {axis: lax.axis_index(axis) for axis in axes}
    near = {}
    for axis in axes:
        size = lax.axis_size(axis)
        near[axis] = (lax.rem(me[axis] + size - 1, size), lax.rem(me[axis] + 1, size))
    mz = me["pz"]
    last = rows - 1

    def row_at(i):
        half, odd_one = i // 2, i % 2
        return half + odd_one * (last - 2 * half)

    def load(which, y):
        if which == 0:
            place = even.at[1 + y, pl.ds(1, width)]
            return pltpu.make_async_copy(tracer.at[y], place, load_sem.at[0, y])
        array, place = ((conductance, cond), (source, src))[which - 1]
        return pltpu.make_async_copy(array.at[y], place.at[y], load_sem.at[which, y])

    def remote(a, b, send, recv, axis, way):
        return pltpu.make_async_remote_copy(
            src_ref=a, dst_ref=b, send_sem=send, recv_sem=recv,
            device_id={axis: near[axis][way]}, device_id_type=MESH,
        )

    def z_copy(par, way, y):
        return remote(
            z_out.at[par, way, y], z_in.at[par, way, y], zs.at[par, way, y], zr.at[par, way, y], "pz", way
        )

    def x_copy(par, way, y):
        field = fields[par]
        mine, theirs = ((1, width + 1), (width, 0))[way]
        return remote(
            field.at[1 + y, mine], field.at[1 + y, theirs], xs.at[par, way, y], xr.at[par, way, y], "px", way
        )

    def y_copy(par, way):
        field = fields[par]
        mine, theirs = ((1, rows + 1), (rows, 0))[way]
        inner = pl.ds(1, width)
        return remote(
            field.at[mine, inner], field.at[theirs, inner], ys.at[par, way], yr.at[par, way], "py", way
        )

    def p_copy(y):
        return remote(p_out.at[y], p_in.at[y], ps.at[y], pr.at[y], "pz", UP)

    def send_row(par, y):
        for way in (DOWN, UP):
            z_copy(par, way, y).start()
        for way in (DOWN, UP):
            x_copy(par, way, y).start()

        @pl.when(y == 0)
        def _():
            y_copy(par, DOWN).start()

        @pl.when(y == last)
        def _():
            y_copy(par, UP).start()

    def sent_row(par, y):
        for way in (DOWN, UP):
            z_copy(par, way, y).wait_send()
            x_copy(par, way, y).wait_send()

        @pl.when(y == 0)
        def _():
            y_copy(par, DOWN).wait_send()

        @pl.when(y == last)
        def _():
            y_copy(par, UP).wait_send()

    def arrived_row(par, y):
        for way in (DOWN, UP):
            x_copy(par, way, y).wait_recv()

        @pl.when(y == 0)
        def _():
            y_copy(par, UP).wait_recv()

        @pl.when(y == last)
        def _():
            y_copy(par, DOWN).wait_recv()

        for way in (DOWN, UP):
            z_copy(par, way, y).wait_recv()

    def each_row(body):
        def run(i, carry):
            body(row_at(i))
            return carry

        lax.fori_loop(0, rows, run, 0)

    def each_slab(body):
        def run(i, carry):
            body(pl.multiple_of(i * SLAB, SLAB))
            return carry

        lax.fori_loop(0, width // SLAB, run, 0)

    for which in (0, 1, 2):
        each_row(lambda y: load(which, y).start())

    barrier = pltpu.get_barrier_semaphore()
    for axis in axes:
        for way in (DOWN, UP):
            pl.semaphore_signal(barrier, inc=1, device_id={axis: near[axis][way]}, device_id_type=MESH)
    pl.semaphore_wait(barrier, 6)

    level = lax.broadcasted_iota(jnp.int32, (8, 128), 0)

    def first(y):
        load(0, y).wait()

        def slab(x0):
            for j in range(SLAB):
                value = even[1 + y, 1 + x0 + j]
                z_out[0, DOWN, y, pl.ds(x0 + j, 1), :] = value[0:1, :]
                z_out[0, UP, y, pl.ds(x0 + j, 1), :] = value[7:8, :]

        each_slab(slab)
        send_row(0, y)

    each_row(first)

    for step in range(1, STEPS + 1):
        old, new = (step - 1) % 2, step % 2
        before, after = fields[old], fields[new]

        def advance(y, step=step, old=old, new=new, before=before, after=after):
            if step == 1:
                load(1, y).wait()
                load(2, y).wait()
            if 2 <= step < STEPS:
                sent_row(new, y)
            arrived_row(old, y)

            def slab(x0):
                line = [before[1 + y, x0 + j] for j in range(SLAB + 2)]
                for j in range(SLAB):
                    x = x0 + j
                    here = line[j + 1]
                    low = z_in[old, UP, y, pl.ds(x, 1), :]
                    high = z_in[old, DOWN, y, pl.ds(x, 1), :]
                    around = (line[j] + line[j + 2]) + (before[y, 1 + x] + before[2 + y, 1 + x])
                    below = pltpu.roll(jnp.where(level == 7, low, here), 1, 0)
                    above = pltpu.roll(jnp.where(level == 0, high, here), 7, 0)
                    spread = around + (below + above) - 6.0 * here
                    value = here + cond[y, x] * spread + src[y, x]
                    if step < STEPS:
                        after[1 + y, 1 + x] = value
                        z_out[new, DOWN, y, pl.ds(x, 1), :] = value[0:1, :]
                        z_out[new, UP, y, pl.ds(x, 1), :] = value[7:8, :]
                    else:
                        end[y, x] = value
                        run = value
                        for shift in (1, 2, 4):
                            run = run + jnp.where(level >= shift, pltpu.roll(run, shift, 0), 0.0)
                        potential[y, x] = run
                        p_out[y, pl.ds(x, 1), :] = run[7:8, :]

            each_slab(slab)
            if step < STEPS:
                send_row(new, y)
            else:

                @pl.when(mz == 0)
                def _():
                    p_copy(y).start()

        each_row(advance)

    def finish(y):
        for par in (0, 1):
            sent_row(par, y)

        @pl.when(mz == 0)
        def _():
            p_in[y] = jnp.zeros_like(p_in[y])

        @pl.when(mz > 0)
        def _():
            p_copy(y).wait_recv()

            @pl.when(mz < zsize - 1)
            def _():
                p_out[y] += p_in[y]
                p_copy(y).start()

        def slab(x0):
            for j in range(SLAB):
                x = x0 + j
                potential[y, x] = (potential[y, x] + p_in[y, pl.ds(x, 1), :]) * (1.0 / total_z)

        each_slab(slab)

    each_row(finish)

    @pl.when(mz < zsize - 1)
    def _():
        each_row(lambda y: p_copy(y).wait_send())


def on_device(tracer, conductance, source):
    rows, width, depth, members = tracer.shape
    zsize = lax.axis_size("pz")
    block = (rows, width, depth, members)
    padded = (rows + 2, width + 2, depth, members)
    face = (rows, width, members)
    f32 = jnp.float32
    dma = pltpu.SemaphoreType.DMA
    cells = rows * width * depth * members
    return pl.pallas_call(
        functools.partial(kernel, rows, width, zsize, depth * zsize),
        out_shape=OUT(block),
        in_specs=[pl.BlockSpec(memory_space=pl.ANY)] * 3,
        out_specs=(pl.BlockSpec(memory_space=pltpu.VMEM),) * 2,
        scratch_shapes=[
            pltpu.VMEM(padded, f32),
            pltpu.VMEM(padded, f32),
            pltpu.VMEM(block, f32),
            pltpu.VMEM(block, f32),
            pltpu.VMEM((2, 2) + face, f32),
            pltpu.VMEM((2, 2) + face, f32),
            pltpu.VMEM(face, f32),
            pltpu.VMEM(face, f32),
            dma((3, rows)),
            dma((2, 2, rows)),
            dma((2, 2, rows)),
            dma((2, 2, rows)),
            dma((2, 2, rows)),
            dma((2, 2)),
            dma((2, 2)),
            dma((rows,)),
            dma((rows,)),
        ],
        compiler_params=pltpu.CompilerParams(
            collective_id=0, has_side_effects=True, vmem_limit_bytes=LIMIT
        ),
        cost_estimate=pl.CostEstimate(flops=48 * cells, bytes_accessed=20 * cells, transcendentals=0),
        name="diffuse",
    )(tracer, conductance, source)


LIMIT = 47 * 2**20


def OUT(block):
    return (pltpu.VMEM(block, jnp.float32), pltpu.VMEM(block, jnp.float32))


def solution(mesh):
    placed = P("py", "px", "pz", None)
    return jax.shard_map(
        on_device,
        mesh=mesh,
        in_specs=(placed, placed, placed),
        out_specs=(placed, placed),
        check_vma=False,
    )
```

profile of v0, /device:TPU:116, one launch (start us, length us, event | category | flops | bytes accessed | tf_op | source)
XLA Modules:
  0.0 133.9 jit_solution(13263763319678948489)
XLA Ops:
  0.6 126.5 %diffuse.1 = (f32[16,128,8,128]{3,2,1,0:T(8,128)S(1)}, f32[16,128,8,128]{3,2,1,0:T(8,128)S(1)}) custom-call(f32[16,128,8,128]{3,2,1,0:T(8,128)} %tracer.1, f32[16,128,8,128]{3,2,1,0:T(8,128)} %conductance.1, f32[16,128,8,128]{3,2,1,0:T(8,128)} %source.1), custom_call_target="tpu_custom_call" | custom-call | flops 100663296 | bytes 41943040 | tf_op jit(solution)/shard_map/diffuse/pallas_call | solution.py:241
  127.1 3.4 %copy.7 = f32[16,128,8,128]{3,2,1,0:T(8,128)} copy(f32[16,128,8,128]{3,2,1,0:T(8,128)S(1)} %get-tuple-element.2) | data formatting | bytes 16777216
  130.5 3.4 %copy.8 = f32[16,128,8,128]{3,2,1,0:T(8,128)} copy(f32[16,128,8,128]{3,2,1,0:T(8,128)S(1)} %get-tuple-element.3) | data formatting | bytes 16777216
where the time goes:
time: 134 us
  Pallas kernels  126 us (94%)
  local copies, waits for them, and re-layouts  6.8 us (5%)
    pallas_call x1, Pallas kernels, on_device(): pl.pallas_call(functools.partial(kernel, rows, width, zsize, depth * zsiz...  126 us
    unnamed x2, local copies, waits for them, and re-layouts  6.8 us

commit v1 on v0

--- a/solution.py
+++ b/solution.py
@@ -12,12 +12,26 @@
 SLAB = 8
 DOWN, UP = 0, 1
 
+KINDS = ("chain", "low", "high", "middle")
+ORIGINS = {
+    "chain": ((UP, (0,)),),
+    "low": ((UP, (1,)), (DOWN, (0,))),
+    "high": ((UP, (0,)), (DOWN, (2,))),
+    "middle": ((UP, (0, 2)), (DOWN, (1,))),
+}
+RELAYS = {
+    "chain": ((UP, (1, 2), ()),),
+    "low": ((UP, (2,), ()), (DOWN, (), (3, 2))),
+    "high": ((UP, (1,), ()), (DOWN, (1, 0), ())),
+    "middle": ((DOWN, (0,), (3,)),),
+}
+
 
 def kernel(
-    rows, width, zsize, total_z,
+    rows, width, total_z,
     tracer, conductance, source,
     potential, end,
-    even, odd, cond, src, z_out, z_in, p_out, p_in,
+    even, odd, cond, src, z_out, z_in, total, p_in,
     load_sem, zs, zr, xs, xr, ys, yr, ps, pr,
 ):
     fields = (even, odd)
@@ -28,7 +42,7 @@
         size = lax.axis_size(axis)
         near[axis] = (lax.rem(me[axis] + size - 1, size), lax.rem(me[axis] + 1, size))
     mz = me["pz"]
-    last = rows - 1
+    last, quarter = rows - 1, rows // 4
 
     def row_at(i):
         half, odd_one = i // 2, i % 2
@@ -67,8 +81,52 @@
             field.at[mine, inner], field.at[theirs, inner], ys.at[par, way], yr.at[par, way], "py", way
         )
 
-    def p_copy(y):
-        return remote(p_out.at[y], p_in.at[y], ps.at[y], pr.at[y], "pz", UP)
+    def p_copy(way, y, place):
+        return remote(place, p_in.at[way, y], ps.at[way, y], pr.at[way, y], "pz", way)
+
+    def p_arrived(way, y):
+        p_copy(way, y, total.at[y]).wait_recv()
+
+    def on(devices):
+        hit = mz == devices[0]
+        for device in devices[1:]:
+            hit = jnp.logical_or(hit, mz == device)
+        return pl.when(hit)
+
+    def originate(kind, y):
+        for way, devices in ORIGINS[kind]:
+
+            @on(devices)
+            def _():
+                p_copy(way, y, total.at[y]).start()
+
+    def relay(kind, way, device, y):
+        adds = [pair[1] for pair in RELAYS[kind] if pair[0] == way][0]
+
+        @on((device,))
+        def _():
+            p_arrived(way, y)
+            if device in adds:
+                z_in[0, way, y] = p_in[way, y] + total[y]
+                p_copy(way, y, z_in.at[0, way, y]).start()
+            else:
+                p_copy(way, y, p_in.at[way, y]).start()
+
+    def conclude(device, y, ways, waits=()):
+        @on((device,))
+        def _():
+            for way in waits:
+                p_arrived(way, y)
+
+            def slab(x0):
+                for j in range(SLAB):
+                    x = x0 + j
+                    below = p_in[ways[0], y, pl.ds(x, 1), :]
+                    for way in ways[1:]:
+                        below = below + p_in[way, y, pl.ds(x, 1), :]
+                    potential[y, x] = potential[y, x] + below * (1.0 / total_z)
+
+            each_slab(slab)
 
     def send_row(par, y):
         for way in (DOWN, UP):
@@ -126,8 +184,7 @@
 
         lax.fori_loop(0, width // SLAB, run, 0)
 
-    for which in (0, 1, 2):
-        each_row(lambda y: load(which, y).start())
+    each_row(lambda y: load(0, y).start())
 
     barrier = pltpu.get_barrier_semaphore()
     for axis in axes:
@@ -139,6 +196,8 @@
 
     def first(y):
         load(0, y).wait()
+        load(1, y).start()
+        load(2, y).start()
 
         def slab(x0):
             for j in range(SLAB):
@@ -184,49 +243,79 @@
                         run = value
                         for shift in (1, 2, 4):
                             run = run + jnp.where(level >= shift, pltpu.roll(run, shift, 0), 0.0)
-                        potential[y, x] = run
-                        p_out[y, pl.ds(x, 1), :] = run[7:8, :]
+                        potential[y, x] = run * (1.0 / total_z)
+                        total[y, pl.ds(x, 1), :] = run[7:8, :]
 
             each_slab(slab)
             if step < STEPS:
                 send_row(new, y)
-            else:
-
-                @pl.when(mz == 0)
-                def _():
-                    p_copy(y).start()
-
-        each_row(advance)
-
-    def finish(y):
-        for par in (0, 1):
-            sent_row(par, y)
-
-        @pl.when(mz == 0)
-        def _():
-            p_in[y] = jnp.zeros_like(p_in[y])
-
-        @pl.when(mz > 0)
-        def _():
-            p_copy(y).wait_recv()
-
-            @pl.when(mz < zsize - 1)
-            def _():
-                p_out[y] += p_in[y]
-                p_copy(y).start()
-
-        def slab(x0):
-            for j in range(SLAB):
-                x = x0 + j
-                potential[y, x] = (potential[y, x] + p_in[y, pl.ds(x, 1), :]) * (1.0 / total_z)
-
-        each_slab(slab)
-
-    each_row(finish)
-
-    @pl.when(mz < zsize - 1)
-    def _():
-        each_row(lambda y: p_copy(y).wait_send())
+
+        if step < STEPS:
+            each_row(advance)
+            continue
+        for place, kind in enumerate(KINDS):
+
+            def run(k, carry, place=place, kind=kind):
+                y = row_at(place * quarter + k)
+                advance(y)
+                originate(kind, y)
+                return carry
+
+            lax.fori_loop(0, quarter, run, 0)
+
+    def each_quarter(body):
+        def run(k, carry):
+            body({kind: row_at(place * quarter + k) for place, kind in enumerate(KINDS)})
+            return carry
+
+        lax.fori_loop(0, quarter, run, 0)
+
+    def first_hops(at):
+        relay("chain", UP, 1, at["chain"])
+        relay("high", DOWN, 1, at["high"])
+        relay("low", UP, 2, at["low"])
+        relay("low", DOWN, 3, at["low"])
+        relay("middle", DOWN, 0, at["middle"])
+        relay("low", DOWN, 2, at["low"])
+        conclude(1, at["chain"], (UP,))
+        conclude(2, at["low"], (UP, DOWN))
+
+    def second_hops(at):
+        relay("high", UP, 1, at["high"])
+        relay("high", DOWN, 0, at["high"])
+        relay("chain", UP, 2, at["chain"])
+        relay("middle", DOWN, 3, at["middle"])
+        for kind in KINDS:
+            for par in (0, 1):
+                sent_row(par, at[kind])
+        conclude(1, at["high"], (UP,))
+        conclude(2, at["chain"], (UP,))
+        conclude(3, at["low"], (UP, DOWN), (UP,))
+        conclude(3, at["middle"], (UP, DOWN), (UP,))
+
+    def third_hops(at):
+        conclude(1, at["low"], (DOWN,), (DOWN,))
+        conclude(2, at["middle"], (DOWN,), (DOWN,))
+
+    def last_hops(at):
+        conclude(1, at["middle"], (UP,), (UP,))
+        conclude(2, at["high"], (UP,), (UP,))
+        conclude(3, at["chain"], (UP,), (UP,))
+        conclude(3, at["high"], (DOWN,), (DOWN,))
+
+    def all_sent(at):
+        for kind in KINDS:
+            for way in (DOWN, UP):
+                devices = sum([pair[1] for pair in ORIGINS[kind] if pair[0] == way], ())
+                devices += sum([pair[1] + pair[2] for pair in RELAYS[kind] if pair[0] == way], ())
+                if devices:
+
+                    @on(devices)
+                    def _():
+                        p_copy(way, at[kind], total.at[at[kind]]).wait_send()
+
+    for body in (first_hops, second_hops, third_hops, last_hops, all_sent):
+        each_quarter(body)
 
 
 def on_device(tracer, conductance, source):
@@ -239,8 +328,8 @@
     dma = pltpu.SemaphoreType.DMA
     cells = rows * width * depth * members
     return pl.pallas_call(
-        functools.partial(kernel, rows, width, zsize, depth * zsize),
-        out_shape=OUT(block),
+        functools.partial(kernel, rows, width, depth * zsize),
+        out_shape=(pltpu.VMEM(block, f32), pltpu.VMEM(block, f32)),
         in_specs=[pl.BlockSpec(memory_space=pl.ANY)] * 3,
         out_specs=(pl.BlockSpec(memory_space=pltpu.VMEM),) * 2,
         scratch_shapes=[
@@ -251,7 +340,7 @@
             pltpu.VMEM((2, 2) + face, f32),
             pltpu.VMEM((2, 2) + face, f32),
             pltpu.VMEM(face, f32),
-            pltpu.VMEM(face, f32),
+            pltpu.VMEM((2,) + face, f32),
             dma((3, rows)),
             dma((2, 2, rows)),
             dma((2, 2, rows)),
@@ -259,22 +348,15 @@
             dma((2, 2, rows)),
             dma((2, 2)),
             dma((2, 2)),
-            dma((rows,)),
-            dma((rows,)),
+            dma((2, rows)),
+            dma((2, rows)),
         ],
         compiler_params=pltpu.CompilerParams(
-            collective_id=0, has_side_effects=True, vmem_limit_bytes=LIMIT
+            collective_id=0, has_side_effects=True, vmem_limit_bytes=47 * 2**20
         ),
         cost_estimate=pl.CostEstimate(flops=48 * cells, bytes_accessed=20 * cells, transcendentals=0),
         name="diffuse",
     )(tracer, conductance, source)
-
-
-LIMIT = 47 * 2**20
-
-
-def OUT(block):
-    return (pltpu.VMEM(block, jnp.float32), pltpu.VMEM(block, jnp.float32))
 
 
 def solution(mesh):

time: 134 us -> 123 us (0.918)
  Pallas kernels: 126 us -> 115 us
    pallas_call x1, Pallas kernels: 126 us -> 115 us  [on_device(): pl.pallas_call(functools.partial(kernel, rows, width, depth * zsize), out...]
where the time goes in v1:
time: 123 us; the launch traced here: 122 us
  Pallas kernels  115 us (93%)
  local copies, waits for them, and re-layouts  6.8 us (6%)
    pallas_call x1, Pallas kernels, on_device(): pl.pallas_call(functools.partial(kernel, rows, width, depth * zsize), out...  115 us
    unnamed x2, local copies, waits for them, and re-layouts  6.8 us

profile of v1, /device:TPU:116, one launch (start us, length us, event | category | flops | bytes accessed | tf_op | source)
XLA Modules:
  0.0 122.3 jit_solution(15920199160209618753)
XLA Ops:
  0.6 114.9 %diffuse.1 = (f32[16,128,8,128]{3,2,1,0:T(8,128)S(1)}, f32[16,128,8,128]{3,2,1,0:T(8,128)S(1)}) custom-call(f32[16,128,8,128]{3,2,1,0:T(8,128)} %tracer.1, f32[16,128,8,128]{3,2,1,0:T(8,128)} %conductance.1, f32[16,128,8,128]{3,2,1,0:T(8,128)} %source.1), custom_call_target="tpu_custom_call" | custom-call | flops 100663296 | bytes 41943040 | tf_op jit(solution)/shard_map/diffuse/pallas_call | solution.py:330
  115.5 3.4 %copy.7 = f32[16,128,8,128]{3,2,1,0:T(8,128)} copy(f32[16,128,8,128]{3,2,1,0:T(8,128)S(1)} %get-tuple-element.2) | data formatting | bytes 16777216
  118.9 3.4 %copy.8 = f32[16,128,8,128]{3,2,1,0:T(8,128)} copy(f32[16,128,8,128]{3,2,1,0:T(8,128)S(1)} %get-tuple-element.3) | data formatting | bytes 16777216

commit v2 on v1

v2 whole, which is shorter than its diff:
```python
import functools

import jax
import jax.numpy as jnp
from jax import lax
from jax.experimental import pallas as pl
from jax.experimental.pallas import tpu as pltpu
from jax.sharding import PartitionSpec as P

MESH = pl.DeviceIdType.MESH
STEPS = 4
SLAB = 8
DOWN, UP = 0, 1

KINDS = ("chain", "low", "high", "middle")
ORIGINS = {
    "chain": ((UP, (0,)),),
    "low": ((UP, (1,)), (DOWN, (0,))),
    "high": ((UP, (0,)), (DOWN, (2,))),
    "middle": ((UP, (0, 2)), (DOWN, (1,))),
}
RELAYS = {
    "chain": ((UP, (1, 2), ()),),
    "low": ((UP, (2,), ()), (DOWN, (), (3, 2))),
    "high": ((UP, (1,), ()), (DOWN, (1, 0), ())),
    "middle": ((DOWN, (0,), (3,)),),
}

LAST = ((1, "middle", UP), (2, "high", UP), (3, "chain", UP), (3, "high", DOWN))


def row_of(rows, i):
    half, odd_one = i // 2, i % 2
    return half + odd_one * (rows - 1 - 2 * half)


def on(mz, devices):
    hit = mz == devices[0]
    for device in devices[1:]:
        hit = jnp.logical_or(hit, mz == device)
    return pl.when(hit)


def add_below(out, base, p_in, y, ways, scale):
    def run(i, carry):
        for j in range(SLAB):
            x = i * SLAB + j
            below = p_in[ways[0], y, pl.ds(x, 1), :]
            for way in ways[1:]:
                below = below + p_in[way, y, pl.ds(x, 1), :]
            out[x] = base[x] + below * scale
        return carry

    lax.fori_loop(0, base.shape[0] // SLAB, run, 0)


def kernel(
    rows, width, total_z,
    tracer, conductance, source,
    potential, end, p_in,
    even, odd, cond, src, z_out, z_in, total,
    load_sem, zs, zr, xs, xr, ys, yr, ps, pr,
):
    fields = (even, odd)
    axes = ("py", "px", "pz")
    me = {axis: lax.axis_index(axis) for axis in axes}
    near = {}
    for axis in axes:
        size = lax.axis_size(axis)
        near[axis] = (lax.rem(me[axis] + size - 1, size), lax.rem(me[axis] + 1, size))
    mz = me["pz"]
    last, quarter = rows - 1, rows // 4
    row_at = functools.partial(row_of, rows)

    def load_field(part):
        place = pl.ds(part * quarter, quarter)
        inside = even.at[pl.ds(1 + part * quarter, quarter), pl.ds(1, width)]
        return pltpu.make_async_copy(tracer.at[place], inside, load_sem.at[part])

    def load_rest():
        return (
            pltpu.make_async_copy(conductance, cond, load_sem.at[4]),
            pltpu.make_async_copy(source, src, load_sem.at[5]),
        )

    def remote(a, b, send, recv, axis, way):
        return pltpu.make_async_remote_copy(
            src_ref=a, dst_ref=b, send_sem=send, recv_sem=recv,
            device_id={axis: near[axis][way]}, device_id_type=MESH,
        )

    def z_copy(par, way, y):
        return remote(z_out.at[par, y, way], z_in.at[par, y, way], zs.at[par], zr.at[par, y], "pz", way)

    def z_all_sent(par):
        remote(z_out.at[par], z_in.at[par], zs.at[par], zr.at[par, 0], "pz", UP).wait_send()

    def z_arrived(par, y):
        remote(z_out.at[par, y], z_in.at[par, y], zs.at[par], zr.at[par, y], "pz", UP).wait_recv()

    def x_copy(par, way):
        field = fields[par]
        mine, theirs = ((1, width + 1), (width, 0))[way]
        inner = pl.ds(1, rows)
        return remote(
            field.at[inner, mine], field.at[inner, theirs], xs.at[par, way], xr.at[par, way], "px", way
        )

    def y_copy(par, way):
        field = fields[par]
        mine, theirs = ((1, rows + 1), (rows, 0))[way]
        inner = pl.ds(1, width)
        return remote(
            field.at[mine, inner], field.at[theirs, inner], ys.at[par, way], yr.at[par, way], "py", way
        )

    def p_copy(kind, way, y, place):
        return remote(place, p_in.at[way, y], ps.at[way, KINDS.index(kind)], pr.at[way, y], "pz", way)

    def p_arrived(way, y):
        p_copy(KINDS[0], way, y, total.at[y]).wait_recv()

    def p_all_sent(kind, way):
        group = pl.ds(0, quarter)
        sem = ps.at[way, KINDS.index(kind)]
        remote(total.at[group], p_in.at[way, group], sem, pr.at[way, 0], "pz", way).wait_send()

    def originate(kind, y):
        for way, devices in ORIGINS[kind]:

            @on(mz, devices)
            def _():
                p_copy(kind, way, y, total.at[y]).start()

    def relay(kind, way, device, y):
        adds = [pair[1] for pair in RELAYS[kind] if pair[0] == way][0]

        @on(mz, (device,))
        def _():
            p_arrived(way, y)
            if device in adds:
                z_in[0, y, way] = p_in[way, y] + total[y]
                p_copy(kind, way, y, z_in.at[0, y, way]).start()
            else:
                p_copy(kind, way, y, p_in.at[way, y]).start()

    def conclude(device, y, ways, waits=()):
        @on(mz, (device,))
        def _():
            for way in waits:
                p_arrived(way, y)

            add_below(potential.at[y], potential.at[y], p_in, y, ways, 1.0 / total_z)

    def send_row(par, y):
        for way in (DOWN, UP):
            z_copy(par, way, y).start()

        @pl.when(y == 0)
        def _():
            y_copy(par, DOWN).start()

        @pl.when(y == last)
        def _():
            y_copy(par, UP).start()

    def all_sent_of(par):
        z_all_sent(par)
        for way in (DOWN, UP):
            x_copy(par, way).wait_send()
            y_copy(par, way).wait_send()

    def arrived_row(par, y):
        @pl.when(y == 0)
        def _():
            y_copy(par, UP).wait_recv()

        @pl.when(y == last)
        def _():
            y_copy(par, DOWN).wait_recv()

        z_arrived(par, y)

    def each_row(body):
        def run(i, carry):
            body(row_at(i))
            return carry

        lax.fori_loop(0, rows, run, 0)

    def each_slab(body):
        def run(i, carry):
            body(pl.multiple_of(i * SLAB, SLAB))
            return carry

        lax.fori_loop(0, width // SLAB, run, 0)

    barrier = pltpu.get_barrier_semaphore()
    for axis in ("pz", "px", "py"):
        for way in (DOWN, UP):
            pl.semaphore_signal(barrier, inc=1, device_id={axis: near[axis][way]}, device_id_type=MESH)

    for part in (0, 3, 1, 2):
        load_field(part).start()

    level = lax.broadcasted_iota(jnp.int32, (8, 128), 0)

    def pack(y):
        def slab(x0):
            for j in range(SLAB):
                value = even[1 + y, 1 + x0 + j]
                z_out[0, y, DOWN, pl.ds(x0 + j, 1), :] = value[0:1, :]
                z_out[0, y, UP, pl.ds(x0 + j, 1), :] = value[7:8, :]

        each_slab(slab)

    def some_rows(low, high, body):
        lax.fori_loop(low, high, lambda i, carry: (body(row_at(i)), carry)[1], 0)

    def first(y):
        pack(y)
        send_row(0, y)

    for part in (0, 3):
        load_field(part).wait()
    for copy in load_rest():
        copy.start()
    some_rows(0, quarter, pack)
    pl.semaphore_wait(barrier, 6)
    some_rows(0, quarter, functools.partial(send_row, 0))
    some_rows(quarter, 2 * quarter, first)
    for part in (1, 2):
        load_field(part).wait()
    some_rows(2 * quarter, rows, first)
    for way in (DOWN, UP):
        x_copy(0, way).start()

    for step in range(1, STEPS + 1):
        old, new = (step - 1) % 2, step % 2
        before, after = fields[old], fields[new]
        if step == 1:
            for copy in load_rest():
                copy.wait()
        if 2 <= step < STEPS:
            all_sent_of(new)
        for way in (DOWN, UP):
            x_copy(old, way).wait_recv()

        def advance(y, step=step, old=old, new=new, before=before, after=after):
            arrived_row(old, y)

            def slab(x0):
                line = [before[1 + y, x0 + j] for j in range(SLAB + 2)]
                for j in range(SLAB):
                    x = x0 + j
                    here = line[j + 1]
                    low = z_in[old, y, UP, pl.ds(x, 1), :]
                    high = z_in[old, y, DOWN, pl.ds(x, 1), :]
                    around = (line[j] + line[j + 2]) + (before[y, 1 + x] + before[2 + y, 1 + x])
                    below = pltpu.roll(jnp.where(level == 7, low, here), 1, 0)
                    above = pltpu.roll(jnp.where(level == 0, high, here), 7, 0)
                    spread = around + (below + above) - 6.0 * here
                    value = here + cond[y, x] * spread + src[y, x]
                    if step < STEPS:
                        after[1 + y, 1 + x] = value
                        z_out[new, y, DOWN, pl.ds(x, 1), :] = value[0:1, :]
                        z_out[new, y, UP, pl.ds(x, 1), :] = value[7:8, :]
                    else:
                        end[y, x] = value
                        run = value
                        for shift in (1, 2, 4):
                            run = run + jnp.where(level >= shift, pltpu.roll(run, shift, 0), 0.0)
                        potential[y, x] = run * (1.0 / total_z)
                        total[y, pl.ds(x, 1), :] = run[7:8, :]

            each_slab(slab)
            if step < STEPS:
                send_row(new, y)

        if step < STEPS:
            each_row(advance)
            for way in (DOWN, UP):
                x_copy(new, way).start()
            continue
        for place, kind in enumerate(KINDS):

            def run(k, carry, place=place, kind=kind):
                y = row_at(place * quarter + k)
                advance(y)
                originate(kind, y)
                return carry

            lax.fori_loop(0, quarter, run, 0)

    def each_quarter(body):
        def run(k, carry):
            body({kind: row_at(place * quarter + k) for place, kind in enumerate(KINDS)})
            return carry

        lax.fori_loop(0, quarter, run, 0)

    def first_hops(at):
        relay("chain", UP, 1, at["chain"])
        relay("high", DOWN, 1, at["high"])
        relay("low", UP, 2, at["low"])
        relay("low", DOWN, 3, at["low"])
        relay("middle", DOWN, 0, at["middle"])
        relay("low", DOWN, 2, at["low"])
        conclude(1, at["chain"], (UP,))
        conclude(2, at["low"], (UP, DOWN))

    def second_hops(at):
        relay("high", UP, 1, at["high"])
        relay("high", DOWN, 0, at["high"])
        relay("chain", UP, 2, at["chain"])
        relay("middle", DOWN, 3, at["middle"])
        conclude(1, at["high"], (UP,))
        conclude(2, at["chain"], (UP,))
        conclude(3, at["low"], (UP, DOWN), (UP,))
        conclude(3, at["middle"], (UP, DOWN), (UP,))

    def third_hops(at):
        conclude(1, at["low"], (DOWN,), (DOWN,))
        conclude(2, at["middle"], (DOWN,), (DOWN,))

    def last_hops(at):
        for device, kind, way in LAST:

            @on(mz, (device,))
            def _():
                p_arrived(way, at[kind])

    each_quarter(first_hops)
    for par in (0, 1):
        all_sent_of(par)
    for body in (second_hops, third_hops, last_hops):
        each_quarter(body)
    for kind in KINDS:
        for way in (DOWN, UP):
            devices = sum([pair[1] for pair in ORIGINS[kind] if pair[0] == way], ())
            devices += sum([pair[1] + pair[2] for pair in RELAYS[kind] if pair[0] == way], ())
            if devices:

                @on(mz, devices)
                def _():
                    p_all_sent(kind, way)


def write_out(total_z, held, end, p_in, potential_out, end_out, added, sem):
    mz = lax.axis_index("pz")
    rows = end.shape[0]
    quarter = rows // 4

    def potential_copy(y, source):
        return pltpu.make_async_copy(source, potential_out.at[y], sem.at[1])

    end_copy = pltpu.make_async_copy(end, end_out, sem.at[0])
    end_copy.start()
    for place, kind in enumerate(KINDS):
        late = [(device, way) for device, other, way in LAST if other == kind]

        def run(k, carry, place=place, late=late):
            i = place * quarter + k
            y = row_of(rows, i)
            plain = mz >= 0
            for device, way in late:
                plain = jnp.logical_and(plain, mz != device)

                @on(mz, (device,))
                def _():
                    add_below(added.at[i], held.at[y], p_in, y, (way,), 1.0 / total_z)
                    potential_copy(y, added.at[i]).start()

            @pl.when(plain)
            def _():
                potential_copy(y, held.at[y]).start()

            return carry

        lax.fori_loop(0, quarter, run, 0)
    pltpu.make_async_copy(held, potential_out, sem.at[1]).wait()
    end_copy.wait()


def on_device(tracer, conductance, source):
    rows, width, depth, members = tracer.shape
    zsize = lax.axis_size("pz")
    block = (rows, width, depth, members)
    padded = (rows + 2, width + 2, depth, members)
    face = (rows, width, members)
    f32 = jnp.float32
    dma = pltpu.SemaphoreType.DMA
    cells = rows * width * depth * members
    held = pl.pallas_call(
        functools.partial(kernel, rows, width, depth * zsize),
        out_shape=(pltpu.VMEM(block, f32), pltpu.VMEM(block, f32), pltpu.VMEM((2,) + face, f32)),
        in_specs=[pl.BlockSpec(memory_space=pl.ANY)] * 3,
        out_specs=(pl.BlockSpec(memory_space=pltpu.VMEM),) * 3,
        scratch_shapes=[
            pltpu.VMEM(padded, f32),
            pltpu.VMEM(padded, f32),
            pltpu.VMEM(block, f32),
            pltpu.VMEM(block, f32),
            pltpu.VMEM((2, rows, 2, width, members), f32),
            pltpu.VMEM((2, rows, 2, width, members), f32),
            pltpu.VMEM(face, f32),
            dma((6,)),
            dma((2,)),
            dma((2, rows)),
            dma((2, 2)),
            dma((2, 2)),
            dma((2, 2)),
            dma((2, 2)),
            dma((2, len(KINDS))),
            dma((2, rows)),
        ],
        compiler_params=pltpu.CompilerParams(
            collective_id=0, has_side_effects=True, vmem_limit_bytes=45 * 2**20
        ),
        cost_estimate=pl.CostEstimate(flops=48 * cells, bytes_accessed=20 * cells, transcendentals=0),
        name="diffuse",
    )(tracer, conductance, source)
    return pl.pallas_call(
        functools.partial(write_out, depth * zsize),
        out_shape=(jax.ShapeDtypeStruct(block, f32),) * 2,
        in_specs=[pl.BlockSpec(memory_space=pltpu.VMEM)] * 3,
        out_specs=(pl.BlockSpec(memory_space=pl.ANY),) * 2,
        scratch_shapes=[pltpu.VMEM(block, f32), dma((2,))],
        compiler_params=pltpu.CompilerParams(vmem_limit_bytes=10 * 2**20),
        cost_estimate=pl.CostEstimate(flops=cells, bytes_accessed=8 * cells, transcendentals=0),
        name="write_out",
    )(*held)


def solution(mesh):
    placed = P("py", "px", "pz", None)
    return jax.shard_map(
        on_device,
        mesh=mesh,
        in_specs=(placed, placed, placed),
        out_specs=(placed, placed),
        check_vma=False,
    )
```

time: 123 us -> 119 us (0.967)
  local copies, waits for them, and re-layouts: 6.8 us -> 0 us
  Pallas kernels: 115 us -> 118 us
    unnamed x2 -> x0, local copies, waits for them, and re-layouts: 6.8 us -> none
    pallas_call x0 -> x1, Pallas kernels: none -> 5.93 us  [on_device(): pl.pallas_call(functools.partial(write_out, depth * zsize), out_shape=(ja...]
    pallas_call x1, Pallas kernels: 115 us -> 112 us  [on_device(): pl.pallas_call(functools.partial(kernel, rows, width, depth * zsize), out...]
where the time goes in v2:
time: 119 us; the launch traced here: 118 us
  Pallas kernels  118 us (99%)
    pallas_call x1, Pallas kernels, on_device(): pl.pallas_call(functools.partial(kernel, rows, width, depth * zsize), out...  112 us
    pallas_call x1, Pallas kernels, on_device(): pl.pallas_call(functools.partial(write_out, depth * zsize), out_shape=(ja...  5.93 us

profile of v2, /device:TPU:116, one launch (start us, length us, event | category | flops | bytes accessed | tf_op | source)
XLA Modules:
  0.0 118.2 jit_solution(9770397156437457274)
XLA Ops:
  0.6 111.6 %diffuse.1 = (f32[16,128,8,128]{3,2,1,0:T(8,128)S(1)}, f32[16,128,8,128]{3,2,1,0:T(8,128)S(1)}, f32[2,16,128,128]{3,2,1,0:T(8,128)S(1)}) custom-call(f32[16,128,8,128]{3,2,1,0:T(8,128)} %tracer.1, f32[16,128,8,128]{3,2,1,0:T(8,128)} %conductance.1, f32[16,128,8,128]{3,2,1,0:T(8,128)} %source.1), custom_call_target="tpu_custom_call" | custom-call | flops 100663296 | bytes 41943040 | tf_op jit(solution)/shard_map/diffuse/pallas_call | solution.py:394
  112.2 5.9 %write_out.1 = (f32[16,128,8,128]{3,2,1,0:T(8,128)}, f32[16,128,8,128]{3,2,1,0:T(8,128)}) custom-call(f32[16,128,8,128]{3,2,1,0:T(8,128)S(1)} %get-tuple-element.5.held, f32[16,128,8,128]{3,2,1,0:T(8,128)S(1)} %get-tuple-element.6.end, f32[2,16,128,128]{3,2,1,0:T(8,128)S(1)} %get-tuple-element.7.p_in), custom_call_target="tpu_custom_call" | custom-call | flops 2097152 | bytes 16777216 | tf_op jit(solution)/shard_map/write_out/pallas_call | solution.py:423

commit v3 on v2

--- a/solution.py
+++ b/solution.py
@@ -72,15 +72,23 @@
     last, quarter = rows - 1, rows // 4
     row_at = functools.partial(row_of, rows)
 
-    def load_field(part):
-        place = pl.ds(part * quarter, quarter)
-        inside = even.at[pl.ds(1 + part * quarter, quarter), pl.ds(1, width)]
-        return pltpu.make_async_copy(tracer.at[place], inside, load_sem.at[part])
+    parts = (((0, 1), (last, 1)), ((1, quarter - 1), (last - quarter + 1, quarter - 1)), ((quarter, 2 * quarter),))
+
+    def rows_copy(start, size, sem):
+        inside = even.at[pl.ds(1 + start, size), pl.ds(1, width)]
+        return pltpu.make_async_copy(tracer.at[pl.ds(start, size)], inside, sem)
+
+    def start_part(part):
+        for start, size in parts[part]:
+            rows_copy(start, size, load_sem.at[part]).start()
+
+    def wait_part(part):
+        rows_copy(0, sum(size for _, size in parts[part]), load_sem.at[part]).wait()
 
     def load_rest():
         return (
-            pltpu.make_async_copy(conductance, cond, load_sem.at[4]),
-            pltpu.make_async_copy(source, src, load_sem.at[5]),
+            pltpu.make_async_copy(conductance, cond, load_sem.at[3]),
+            pltpu.make_async_copy(source, src, load_sem.at[4]),
         )
 
     def remote(a, b, send, recv, axis, way):
@@ -89,41 +97,69 @@
             device_id={axis: near[axis][way]}, device_id_type=MESH,
         )
 
+    def z_sem(par, y):
+        index = turn_of(y)
+        return zr.at[index // quarter] if par == 0 else zr.at[4 + index]
+
+    def turn_of(y):
+        far = y // (rows // 2)
+        return 2 * (y + far * (last - 2 * y)) + far
+
     def z_copy(par, way, y):
-        return remote(z_out.at[par, y, way], z_in.at[par, y, way], zs.at[par], zr.at[par, y], "pz", way)
+        return remote(z_out.at[par, y, way], z_in.at[par, y, way], zs.at[par], z_sem(par, y), "pz", way)
 
     def z_all_sent(par):
-        remote(z_out.at[par], z_in.at[par], zs.at[par], zr.at[par, 0], "pz", UP).wait_send()
+        remote(z_out.at[par], z_in.at[par], zs.at[par], zr.at[0], "pz", UP).wait_send()
 
     def z_arrived(par, y):
-        remote(z_out.at[par, y], z_in.at[par, y], zs.at[par], zr.at[par, y], "pz", UP).wait_recv()
+        if par == 1:
+            remote(z_out.at[par, y], z_in.at[par, y], zs.at[par], z_sem(par, y), "pz", UP).wait_recv()
+            return
+        group = pl.ds(0, quarter)
+
+        @pl.when(turn_of(y) % quarter == 0)
+        def _():
+            remote(z_out.at[par, group], z_in.at[par, group], zs.at[par], z_sem(par, y), "pz", UP).wait_recv()
 
     def x_copy(par, way):
         field = fields[par]
         mine, theirs = ((1, width + 1), (width, 0))[way]
         inner = pl.ds(1, rows)
-        return remote(
-            field.at[inner, mine], field.at[inner, theirs], xs.at[par, way], xr.at[par, way], "px", way
-        )
+        return remote(field.at[inner, mine], field.at[inner, theirs], xs.at[par], xr.at[par], "px", way)
+
+    def x_both(par):
+        place = fields[par].at[pl.ds(1, rows), pl.ds(0, 2)]
+        return remote(place, place, xs.at[par], xr.at[par], "px", UP)
 
     def y_copy(par, way):
         field = fields[par]
         mine, theirs = ((1, rows + 1), (rows, 0))[way]
         inner = pl.ds(1, width)
-        return remote(
-            field.at[mine, inner], field.at[theirs, inner], ys.at[par, way], yr.at[par, way], "py", way
-        )
+        return remote(field.at[mine, inner], field.at[theirs, inner], ys.at[par], yr.at[par], "py", way)
+
+    def y_both(par):
+        place = fields[par].at[pl.ds(0, 2), pl.ds(1, width)]
+        return remote(place, place, ys.at[par], yr.at[par], "py", UP)
 
     def p_copy(kind, way, y, place):
-        return remote(place, p_in.at[way, y], ps.at[way, KINDS.index(kind)], pr.at[way, y], "pz", way)
+        return remote(place, p_in.at[way, y], ps.at[way], pr.at[way, y], "pz", way)
 
     def p_arrived(way, y):
         p_copy(KINDS[0], way, y, total.at[y]).wait_recv()
 
-    def p_all_sent(kind, way):
-        group = pl.ds(0, quarter)
-        sem = ps.at[way, KINDS.index(kind)]
-        remote(total.at[group], p_in.at[way, group], sem, pr.at[way, 0], "pz", way).wait_send()
+    def p_all_sent(way, device):
+        count = sum(
+            quarter
+            for kind in KINDS
+            for other, *groups in ORIGINS[kind] + RELAYS[kind]
+            if other == way and device in sum(groups, ())
+        )
+        if count:
+
+            @on(mz, (device,))
+            def _():
+                group = pl.ds(0, count)
+                remote(total.at[group], p_in.at[way, group], ps.at[way], pr.at[way, 0], "pz", way).wait_send()
 
     def originate(kind, y):
         for way, devices in ORIGINS[kind]:
@@ -166,18 +202,13 @@
 
     def all_sent_of(par):
         z_all_sent(par)
-        for way in (DOWN, UP):
-            x_copy(par, way).wait_send()
-            y_copy(par, way).wait_send()
+        x_both(par).wait_send()
+        y_both(par).wait_send()
 
     def arrived_row(par, y):
         @pl.when(y == 0)
         def _():
-            y_copy(par, UP).wait_recv()
-
-        @pl.when(y == last)
-        def _():
-            y_copy(par, DOWN).wait_recv()
+            y_both(par).wait_recv()
 
         z_arrived(par, y)
 
@@ -200,8 +231,8 @@
         for way in (DOWN, UP):
             pl.semaphore_signal(barrier, inc=1, device_id={axis: near[axis][way]}, device_id_type=MESH)
 
-    for part in (0, 3, 1, 2):
-        load_field(part).start()
+    for part in range(len(parts)):
+        start_part(part)
 
     level = lax.broadcasted_iota(jnp.int32, (8, 128), 0)
 
@@ -221,16 +252,15 @@
         pack(y)
         send_row(0, y)
 
-    for part in (0, 3):
-        load_field(part).wait()
+    wait_part(0)
+    some_rows(0, 2, pack)
+    pl.semaphore_wait(barrier, 6)
+    some_rows(0, 2, functools.partial(send_row, 0))
+    wait_part(1)
+    some_rows(2, 2 * quarter, first)
+    wait_part(2)
     for copy in load_rest():
         copy.start()
-    some_rows(0, quarter, pack)
-    pl.semaphore_wait(barrier, 6)
-    some_rows(0, quarter, functools.partial(send_row, 0))
-    some_rows(quarter, 2 * quarter, first)
-    for part in (1, 2):
-        load_field(part).wait()
     some_rows(2 * quarter, rows, first)
     for way in (DOWN, UP):
         x_copy(0, way).start()
@@ -243,8 +273,7 @@
                 copy.wait()
         if 2 <= step < STEPS:
             all_sent_of(new)
-        for way in (DOWN, UP):
-            x_copy(old, way).wait_recv()
+        x_both(old).wait_recv()
 
         def advance(y, step=step, old=old, new=new, before=before, after=after):
             arrived_row(old, y)
@@ -335,15 +364,9 @@
         all_sent_of(par)
     for body in (second_hops, third_hops, last_hops):
         each_quarter(body)
-    for kind in KINDS:
+    for device in range(4):
         for way in (DOWN, UP):
-            devices = sum([pair[1] for pair in ORIGINS[kind] if pair[0] == way], ())
-            devices += sum([pair[1] + pair[2] for pair in RELAYS[kind] if pair[0] == way], ())
-            if devices:
-
-                @on(mz, devices)
-                def _():
-                    p_all_sent(kind, way)
+            p_all_sent(way, device)
 
 
 def write_out(total_z, held, end, p_in, potential_out, end_out, added, sem):
@@ -355,7 +378,9 @@
         return pltpu.make_async_copy(source, potential_out.at[y], sem.at[1])
 
     end_copy = pltpu.make_async_copy(end, end_out, sem.at[0])
-    end_copy.start()
+    for place in range(4):
+        part = pl.ds(place * quarter, quarter)
+        pltpu.make_async_copy(end.at[part], end_out.at[part], sem.at[0]).start()
     for place, kind in enumerate(KINDS):
         late = [(device, way) for device, other, way in LAST if other == kind]
 
@@ -404,14 +429,14 @@
             pltpu.VMEM((2, rows, 2, width, members), f32),
             pltpu.VMEM((2, rows, 2, width, members), f32),
             pltpu.VMEM(face, f32),
-            dma((6,)),
-            dma((2,)),
-            dma((2, rows)),
-            dma((2, 2)),
-            dma((2, 2)),
-            dma((2, 2)),
-            dma((2, 2)),
-            dma((2, len(KINDS))),
+            dma((5,)),
+            dma((2,)),
+            dma((4 + rows,)),
+            dma((2,)),
+            dma((2,)),
+            dma((2,)),
+            dma((2,)),
+            dma((2,)),
             dma((2, rows)),
         ],
         compiler_params=pltpu.CompilerParams(

time: 119 us -> 119 us (level)
  no operation moved by 1% of the time
where the time goes in v3:
time: 119 us; the launch traced here: 118 us
  Pallas kernels  117 us (98%)
    pallas_call x1, Pallas kernels, on_device(): pl.pallas_call(functools.partial(kernel, rows, width, depth * zsize), out...  111 us
    pallas_call x1, Pallas kernels, on_device(): pl.pallas_call(functools.partial(write_out, depth * zsize), out_shape=(ja...  5.82 us

profile of v3, /device:TPU:116, one launch (start us, length us, event | category | flops | bytes accessed | tf_op | source)
XLA Modules:
  0.0 117.8 jit_solution(10567176134729265061)
XLA Ops:
  0.6 111.4 %diffuse.1 = (f32[16,128,8,128]{3,2,1,0:T(8,128)S(1)}, f32[16,128,8,128]{3,2,1,0:T(8,128)S(1)}, f32[2,16,128,128]{3,2,1,0:T(8,128)S(1)}) custom-call(f32[16,128,8,128]{3,2,1,0:T(8,128)} %tracer.1, f32[16,128,8,128]{3,2,1,0:T(8,128)} %conductance.1, f32[16,128,8,128]{3,2,1,0:T(8,128)} %source.1), custom_call_target="tpu_custom_call" | custom-call | flops 100663296 | bytes 41943040 | tf_op jit(solution)/shard_map/diffuse/pallas_call | solution.py:419
  112.0 5.8 %write_out.1 = (f32[16,128,8,128]{3,2,1,0:T(8,128)}, f32[16,128,8,128]{3,2,1,0:T(8,128)}) custom-call(f32[16,128,8,128]{3,2,1,0:T(8,128)S(1)} %get-tuple-element.5.held, f32[16,128,8,128]{3,2,1,0:T(8,128)S(1)} %get-tuple-element.6.end, f32[2,16,128,128]{3,2,1,0:T(8,128)S(1)} %get-tuple-element.7.p_in), custom_call_target="tpu_custom_call" | custom-call | flops 2097152 | bytes 16777216 | tf_op jit(solution)/shard_map/write_out/pallas_call | solution.py:448

commit v4 on v3

--- a/solution.py
+++ b/solution.py
@@ -12,21 +12,41 @@
 SLAB = 8
 DOWN, UP = 0, 1
 
-KINDS = ("chain", "low", "high", "middle")
+SHARES = {"chain": 5, "two": 2, "one": 2, "low": 3, "high": 3, "middle": 1}
 ORIGINS = {
     "chain": ((UP, (0,)),),
+    "two": ((DOWN, (2,)),),
+    "one": ((DOWN, (1,)), (UP, (2,))),
     "low": ((UP, (1,)), (DOWN, (0,))),
     "high": ((UP, (0,)), (DOWN, (2,))),
     "middle": ((UP, (0, 2)), (DOWN, (1,))),
 }
+LATE_ORIGINS = {"two": ((UP, (0,)),)}
 RELAYS = {
     "chain": ((UP, (1, 2), ()),),
+    "two": ((DOWN, (1, 0), (3,)),),
+    "one": ((DOWN, (0,), (3, 2)),),
     "low": ((UP, (2,), ()), (DOWN, (), (3, 2))),
     "high": ((UP, (1,), ()), (DOWN, (1, 0), ())),
     "middle": ((DOWN, (0,), (3,)),),
 }
-
-LAST = ((1, "middle", UP), (2, "high", UP), (3, "chain", UP), (3, "high", DOWN))
+LAST = {
+    (1, "one"): (DOWN, True),
+    (1, "middle"): (UP, False),
+    (1, "two"): (UP, False),
+    (2, "high"): (UP, False),
+    (2, "two"): (DOWN, True),
+    (3, "chain"): (UP, False),
+    (3, "high"): (DOWN, False),
+}
+
+
+def groups_of(rows):
+    start, groups = 0, {}
+    for kind, share in SHARES.items():
+        groups[kind] = (start, start + share * rows // 16)
+        start = groups[kind][1]
+    return groups
 
 
 def row_of(rows, i):
@@ -41,13 +61,15 @@
     return pl.when(hit)
 
 
-def add_below(out, base, p_in, y, ways, scale):
+def add_below(out, base, p_in, y, ways, scale, own=None):
     def run(i, carry):
         for j in range(SLAB):
             x = i * SLAB + j
             below = p_in[ways[0], y, pl.ds(x, 1), :]
             for way in ways[1:]:
                 below = below + p_in[way, y, pl.ds(x, 1), :]
+            if own is not None:
+                below = below - own[y, pl.ds(x, 1), :]
             out[x] = base[x] + below * scale
         return carry
 
@@ -57,8 +79,8 @@
 def kernel(
     rows, width, total_z,
     tracer, conductance, source,
-    potential, end, p_in,
-    even, odd, cond, src, z_out, z_in, total,
+    potential, end, p_in, total,
+    even, odd, cond, src, z_out, z_in,
     load_sem, zs, zr, xs, xr, ys, yr, ps, pr,
 ):
     fields = (even, odd)
@@ -141,18 +163,20 @@
         place = fields[par].at[pl.ds(0, 2), pl.ds(1, width)]
         return remote(place, place, ys.at[par], yr.at[par], "py", UP)
 
-    def p_copy(kind, way, y, place):
+    def p_copy(way, y, place):
         return remote(place, p_in.at[way, y], ps.at[way], pr.at[way, y], "pz", way)
 
     def p_arrived(way, y):
-        p_copy(KINDS[0], way, y, total.at[y]).wait_recv()
+        p_copy(way, y, total.at[y]).wait_recv()
+
+    groups = groups_of(rows)
 
     def p_all_sent(way, device):
         count = sum(
-            quarter
-            for kind in KINDS
-            for other, *groups in ORIGINS[kind] + RELAYS[kind]
-            if other == way and device in sum(groups, ())
+            groups[kind][1] - groups[kind][0]
+            for kind in SHARES
+            for other, *devices in ORIGINS[kind] + LATE_ORIGINS.get(kind, ()) + RELAYS[kind]
+            if other == way and device in sum(devices, ())
         )
         if count:
 
@@ -161,32 +185,28 @@
                 group = pl.ds(0, count)
                 remote(total.at[group], p_in.at[way, group], ps.at[way], pr.at[way, 0], "pz", way).wait_send()
 
-    def originate(kind, y):
-        for way, devices in ORIGINS[kind]:
+    def originate(origins, y):
+        for way, devices in origins:
 
             @on(mz, devices)
             def _():
-                p_copy(kind, way, y, total.at[y]).start()
-
-    def relay(kind, way, device, y):
+                p_copy(way, y, total.at[y]).start()
+
+    def relay(kind, way, device, k):
+        y = row_at(groups[kind][0] + k)
         adds = [pair[1] for pair in RELAYS[kind] if pair[0] == way][0]
-
-        @on(mz, (device,))
-        def _():
+        p_arrived(way, y)
+        if device in adds:
+            z_in[0, y, way] = p_in[way, y] + total[y]
+            p_copy(way, y, z_in.at[0, y, way]).start()
+        else:
+            p_copy(way, y, p_in.at[way, y]).start()
+
+    def conclude(kind, k, ways, waits=()):
+        y = row_at(groups[kind][0] + k)
+        for way in waits:
             p_arrived(way, y)
-            if device in adds:
-                z_in[0, y, way] = p_in[way, y] + total[y]
-                p_copy(kind, way, y, z_in.at[0, y, way]).start()
-            else:
-                p_copy(kind, way, y, p_in.at[way, y]).start()
-
-    def conclude(device, y, ways, waits=()):
-        @on(mz, (device,))
-        def _():
-            for way in waits:
-                p_arrived(way, y)
-
-            add_below(potential.at[y], potential.at[y], p_in, y, ways, 1.0 / total_z)
+        add_below(potential.at[y], potential.at[y], p_in, y, ways, 1.0 / total_z)
 
     def send_row(par, y):
         for way in (DOWN, UP):
@@ -311,65 +331,87 @@
             for way in (DOWN, UP):
                 x_copy(new, way).start()
             continue
-        for place, kind in enumerate(KINDS):
-
-            def run(k, carry, place=place, kind=kind):
-                y = row_at(place * quarter + k)
+        for kind, (low, high) in groups.items():
+
+            def last_step(i, carry, kind=kind):
+                y = row_at(i)
                 advance(y)
-                originate(kind, y)
+                originate(ORIGINS[kind], y)
                 return carry
 
-            lax.fori_loop(0, quarter, run, 0)
-
-    def each_quarter(body):
-        def run(k, carry):
-            body({kind: row_at(place * quarter + k) for place, kind in enumerate(KINDS)})
-            return carry
-
-        lax.fori_loop(0, quarter, run, 0)
-
-    def first_hops(at):
-        relay("chain", UP, 1, at["chain"])
-        relay("high", DOWN, 1, at["high"])
-        relay("low", UP, 2, at["low"])
-        relay("low", DOWN, 3, at["low"])
-        relay("middle", DOWN, 0, at["middle"])
-        relay("low", DOWN, 2, at["low"])
-        conclude(1, at["chain"], (UP,))
-        conclude(2, at["low"], (UP, DOWN))
-
-    def second_hops(at):
-        relay("high", UP, 1, at["high"])
-        relay("high", DOWN, 0, at["high"])
-        relay("chain", UP, 2, at["chain"])
-        relay("middle", DOWN, 3, at["middle"])
-        conclude(1, at["high"], (UP,))
-        conclude(2, at["chain"], (UP,))
-        conclude(3, at["low"], (UP, DOWN), (UP,))
-        conclude(3, at["middle"], (UP, DOWN), (UP,))
-
-    def third_hops(at):
-        conclude(1, at["low"], (DOWN,), (DOWN,))
-        conclude(2, at["middle"], (DOWN,), (DOWN,))
-
-    def last_hops(at):
-        for device, kind, way in LAST:
-
-            @on(mz, (device,))
-            def _():
-                p_arrived(way, at[kind])
-
-    each_quarter(first_hops)
+            lax.fori_loop(low, high, last_step, 0)
+        for kind, origins in LATE_ORIGINS.items():
+            for i in range(*groups[kind]):
+                originate(origins, row_at(i))
+
+    def each(kind):
+        return range(groups[kind][1] - groups[kind][0])
+
+    @on(mz, (0,))
+    def _():
+        for kind in ("one", "middle", "two", "high"):
+            for k in each(kind):
+                relay(kind, DOWN, 0, k)
+
+    @on(mz, (1,))
+    def _():
+        downs = [(kind, k) for kind in ("two", "high") for k in each(kind)]
+        for k in each("chain"):
+            relay("chain", UP, 1, k)
+            if k < len(downs):
+                relay(downs[k][0], DOWN, 1, downs[k][1])
+        for k in each("chain"):
+            conclude("chain", k, (UP,))
+        for k in each("high"):
+            relay("high", UP, 1, k)
+            conclude("high", k, (UP,))
+        for k in each("low"):
+            conclude("low", k, (DOWN,), (DOWN,))
+
+    @on(mz, (2,))
+    def _():
+        for k in each("low"):
+            relay("low", UP, 2, k)
+        downs = [(kind, k) for kind in ("low", "one") for k in each(kind)]
+        for k in each("chain"):
+            if k < len(downs):
+                relay(downs[k][0], DOWN, 2, downs[k][1])
+            relay("chain", UP, 2, k)
+        for k in each("low"):
+            conclude("low", k, (UP, DOWN))
+        for k in each("chain"):
+            conclude("chain", k, (UP,))
+        for k in each("one"):
+            conclude("one", k, (DOWN,))
+        for k in each("middle"):
+            conclude("middle", k, (DOWN,), (DOWN,))
+
+    @on(mz, (3,))
+    def _():
+        for kind in ("low", "one", "middle", "two"):
+            for k in each(kind):
+                relay(kind, DOWN, 3, k)
+        for kind in ("one", "middle", "low"):
+            for k in each(kind):
+                conclude(kind, k, (UP, DOWN), (UP,))
+        for k in each("two"):
+            conclude("two", k, (DOWN,))
+
+    for (device, kind), (way, _) in LAST.items():
+
+        @on(mz, (device,))
+        def _():
+            for i in range(*groups[kind]):
+                p_arrived(way, row_at(i))
+
     for par in (0, 1):
         all_sent_of(par)
-    for body in (second_hops, third_hops, last_hops):
-        each_quarter(body)
     for device in range(4):
         for way in (DOWN, UP):
             p_all_sent(way, device)
 
 
-def write_out(total_z, held, end, p_in, potential_out, end_out, added, sem):
+def write_out(total_z, held, end, p_in, total, potential_out, end_out, added, sem):
     mz = lax.axis_index("pz")
     rows = end.shape[0]
     quarter = rows // 4
@@ -381,19 +423,19 @@
     for place in range(4):
         part = pl.ds(place * quarter, quarter)
         pltpu.make_async_copy(end.at[part], end_out.at[part], sem.at[0]).start()
-    for place, kind in enumerate(KINDS):
-        late = [(device, way) for device, other, way in LAST if other == kind]
-
-        def run(k, carry, place=place, late=late):
-            i = place * quarter + k
+    for kind, (low, high) in groups_of(rows).items():
+        late = [(device, *how) for (device, other), how in LAST.items() if other == kind]
+
+        def run(i, carry, late=late):
             y = row_of(rows, i)
             plain = mz >= 0
-            for device, way in late:
+            for device, way, off in late:
                 plain = jnp.logical_and(plain, mz != device)
 
                 @on(mz, (device,))
                 def _():
-                    add_below(added.at[i], held.at[y], p_in, y, (way,), 1.0 / total_z)
+                    own = total if off else None
+                    add_below(added.at[i], held.at[y], p_in, y, (way,), 1.0 / total_z, own)
                     potential_copy(y, added.at[i]).start()
 
             @pl.when(plain)
@@ -402,7 +444,7 @@
 
             return carry
 
-        lax.fori_loop(0, quarter, run, 0)
+        lax.fori_loop(low, high, run, 0)
     pltpu.make_async_copy(held, potential_out, sem.at[1]).wait()
     end_copy.wait()
 
@@ -418,9 +460,9 @@
     cells = rows * width * depth * members
     held = pl.pallas_call(
         functools.partial(kernel, rows, width, depth * zsize),
-        out_shape=(pltpu.VMEM(block, f32), pltpu.VMEM(block, f32), pltpu.VMEM((2,) + face, f32)),
+        out_shape=(pltpu.VMEM(block, f32), pltpu.VMEM(block, f32), pltpu.VMEM((2,) + face, f32), pltpu.VMEM(face, f32)),
         in_specs=[pl.BlockSpec(memory_space=pl.ANY)] * 3,
-        out_specs=(pl.BlockSpec(memory_space=pltpu.VMEM),) * 3,
+        out_specs=(pl.BlockSpec(memory_space=pltpu.VMEM),) * 4,
         scratch_shapes=[
             pltpu.VMEM(padded, f32),
             pltpu.VMEM(padded, f32),
@@ -428,7 +470,6 @@
             pltpu.VMEM(block, f32),
             pltpu.VMEM((2, rows, 2, width, members), f32),
             pltpu.VMEM((2, rows, 2, width, members), f32),
-            pltpu.VMEM(face, f32),
             dma((5,)),
             dma((2,)),
             dma((4 + rows,)),
@@ -440,7 +481,7 @@
             dma((2, rows)),
         ],
         compiler_params=pltpu.CompilerParams(
-            collective_id=0, has_side_effects=True, vmem_limit_bytes=45 * 2**20
+            collective_id=0, has_side_effects=True, vmem_limit_bytes=44 * 2**20
         ),
         cost_estimate=pl.CostEstimate(flops=48 * cells, bytes_accessed=20 * cells, transcendentals=0),
         name="diffuse",
@@ -448,7 +489,7 @@
     return pl.pallas_call(
         functools.partial(write_out, depth * zsize),
         out_shape=(jax.ShapeDtypeStruct(block, f32),) * 2,
-        in_specs=[pl.BlockSpec(memory_space=pltpu.VMEM)] * 3,
+        in_specs=[pl.BlockSpec(memory_space=pltpu.VMEM)] * 4,
         out_specs=(pl.BlockSpec(memory_space=pl.ANY),) * 2,
         scratch_shapes=[pltpu.VMEM(block, f32), dma((2,))],
         compiler_params=pltpu.CompilerParams(vmem_limit_bytes=10 * 2**20),

time: 119 us -> 118 us (level)
    pallas_call x1, Pallas kernels: 111 us -> 110 us  [on_device(): pl.pallas_call(functools.partial(kernel, rows, width, depth * zsize), out...]
where the time goes in v4:
time: 118 us; the launch traced here: 116 us
  Pallas kernels  116 us (98%)
    pallas_call x1, Pallas kernels, on_device(): pl.pallas_call(functools.partial(kernel, rows, width, depth * zsize), out...  110 us
    pallas_call x1, Pallas kernels, on_device(): pl.pallas_call(functools.partial(write_out, depth * zsize), out_shape=(ja...  5.82 us

profile of v4, /device:TPU:116, one launch (start us, length us, event | category | flops | bytes accessed | tf_op | source)
XLA Modules:
  0.0 116.2 jit_solution(18330933157362857534)
XLA Ops:
  0.6 109.7 %diffuse.1 = (f32[16,128,8,128]{3,2,1,0:T(8,128)S(1)}, f32[16,128,8,128]{3,2,1,0:T(8,128)S(1)}, f32[2,16,128,128]{3,2,1,0:T(8,128)S(1)}, f32[16,128,128]{2,1,0:T(8,128)S(1)}) custom-call(f32[16,128,8,128]{3,2,1,0:T(8,128)} %tracer.1, f32[16,128,8,128]{3,2,1,0:T(8,128)} %conductance.1, f32[16,128,8,128]{3,2,1,0:T(8,128)} %source.1), custom_call_target="tpu_custom_call" | custom-call | flops 100663296 | bytes 41943040 | tf_op jit(solution)/shard_map/diffuse/pallas_call | solution.py:461
  110.3 5.8 %write_out.1 = (f32[16,128,8,128]{3,2,1,0:T(8,128)}, f32[16,128,8,128]{3,2,1,0:T(8,128)}) custom-call(f32[16,128,8,128]{3,2,1,0:T(8,128)S(1)} %get-tuple-element.6.held, f32[16,128,8,128]{3,2,1,0:T(8,128)S(1)} %get-tuple-element.7.end, f32[2,16,128,128]{3,2,1,0:T(8,128)S(1)} %get-tuple-element.8.p_in, f32[16,128,128]{2,1,0:T(8,128)S(1)} %get-tuple-element.9.total), custom_call_target="tpu_custom_call" | custom-call | flops 2097152 | bytes 16777216 | tf_op jit(solution)/shard_map/write_out/pallas_call | solution.py:489

commit v5 on v4

--- a/solution.py
+++ b/solution.py
@@ -12,7 +12,7 @@
 SLAB = 8
 DOWN, UP = 0, 1
 
-SHARES = {"chain": 5, "two": 2, "one": 2, "low": 3, "high": 3, "middle": 1}
+SHARES = {"chain": 5, "low": 3, "one": 2, "two": 2, "high": 3, "middle": 1}
 ORIGINS = {
     "chain": ((UP, (0,)),),
     "two": ((DOWN, (2,)),),
@@ -374,9 +374,9 @@
             relay("low", UP, 2, k)
         downs = [(kind, k) for kind in ("low", "one") for k in each(kind)]
         for k in each("chain"):
+            relay("chain", UP, 2, k)
             if k < len(downs):
                 relay(downs[k][0], DOWN, 2, downs[k][1])
-            relay("chain", UP, 2, k)
         for k in each("low"):
             conclude("low", k, (UP, DOWN))
         for k in each("chain"):

time: 118 us -> 118 us (level)
  no operation moved by 1% of the time
where the time goes in v5:
time: 118 us; the launch traced here: 116 us
  Pallas kernels  116 us (98%)
    pallas_call x1, Pallas kernels, on_device(): pl.pallas_call(functools.partial(kernel, rows, width, depth * zsize), out...  110 us
    pallas_call x1, Pallas kernels, on_device(): pl.pallas_call(functools.partial(write_out, depth * zsize), out_shape=(ja...  5.82 us

profile of v5, /device:TPU:116, one launch (start us, length us, event | category | flops | bytes accessed | tf_op | source)
XLA Modules:
  0.0 116.2 jit_solution(9106321110799555388)
XLA Ops:
  0.6 109.7 %diffuse.1 = (f32[16,128,8,128]{3,2,1,0:T(8,128)S(1)}, f32[16,128,8,128]{3,2,1,0:T(8,128)S(1)}, f32[2,16,128,128]{3,2,1,0:T(8,128)S(1)}, f32[16,128,128]{2,1,0:T(8,128)S(1)}) custom-call(f32[16,128,8,128]{3,2,1,0:T(8,128)} %tracer.1, f32[16,128,8,128]{3,2,1,0:T(8,128)} %conductance.1, f32[16,128,8,128]{3,2,1,0:T(8,128)} %source.1), custom_call_target="tpu_custom_call" | custom-call | flops 100663296 | bytes 41943040 | tf_op jit(solution)/shard_map/diffuse/pallas_call | solution.py:461
  110.3 5.8 %write_out.1 = (f32[16,128,8,128]{3,2,1,0:T(8,128)}, f32[16,128,8,128]{3,2,1,0:T(8,128)}) custom-call(f32[16,128,8,128]{3,2,1,0:T(8,128)S(1)} %get-tuple-element.6.held, f32[16,128,8,128]{3,2,1,0:T(8,128)S(1)} %get-tuple-element.7.end, f32[2,16,128,128]{3,2,1,0:T(8,128)S(1)} %get-tuple-element.8.p_in, f32[16,128,128]{2,1,0:T(8,128)S(1)} %get-tuple-element.9.total), custom_call_target="tpu_custom_call" | custom-call | flops 2097152 | bytes 16777216 | tf_op jit(solution)/shard_map/write_out/pallas_call | solution.py:489

commit v6 on v5

--- a/solution.py
+++ b/solution.py
@@ -9,7 +9,7 @@
 
 MESH = pl.DeviceIdType.MESH
 STEPS = 4
-SLAB = 8
+SLAB = 16
 DOWN, UP = 0, 1
 
 SHARES = {"chain": 5, "low": 3, "one": 2, "two": 2, "high": 3, "middle": 1}

time: 118 us -> 118 us (level)
  no operation moved by 1% of the time
where the time goes in v6:
time: 118 us; the launch traced here: 116 us
  Pallas kernels  116 us (98%)
    pallas_call x1, Pallas kernels, on_device(): pl.pallas_call(functools.partial(kernel, rows, width, depth * zsize), out...  110 us
    pallas_call x1, Pallas kernels, on_device(): pl.pallas_call(functools.partial(write_out, depth * zsize), out_shape=(ja...  5.82 us

profile of v6, /device:TPU:116, one launch (start us, length us, event | category | flops | bytes accessed | tf_op | source)
XLA Modules:
  0.0 116.2 jit_solution(18207613508031397098)
XLA Ops:
  0.6 109.7 %diffuse.1 = (f32[16,128,8,128]{3,2,1,0:T(8,128)S(1)}, f32[16,128,8,128]{3,2,1,0:T(8,128)S(1)}, f32[2,16,128,128]{3,2,1,0:T(8,128)S(1)}, f32[16,128,128]{2,1,0:T(8,128)S(1)}) custom-call(f32[16,128,8,128]{3,2,1,0:T(8,128)} %tracer.1, f32[16,128,8,128]{3,2,1,0:T(8,128)} %conductance.1, f32[16,128,8,128]{3,2,1,0:T(8,128)} %source.1), custom_call_target="tpu_custom_call" | custom-call | flops 100663296 | bytes 41943040 | tf_op jit(solution)/shard_map/diffuse/pallas_call | solution.py:461
  110.3 5.8 %write_out.1 = (f32[16,128,8,128]{3,2,1,0:T(8,128)}, f32[16,128,8,128]{3,2,1,0:T(8,128)}) custom-call(f32[16,128,8,128]{3,2,1,0:T(8,128)S(1)} %get-tuple-element.6.held, f32[16,128,8,128]{3,2,1,0:T(8,128)S(1)} %get-tuple-element.7.end, f32[2,16,128,128]{3,2,1,0:T(8,128)S(1)} %get-tuple-element.8.p_in, f32[16,128,128]{2,1,0:T(8,128)S(1)} %get-tuple-element.9.total), custom_call_target="tpu_custom_call" | custom-call | flops 2097152 | bytes 16777216 | tf_op jit(solution)/shard_map/write_out/pallas_call | solution.py:489
